TPU v7x, 32 devices: a whole 2x2x4 slice. The times are simulated.
32 devices in a mesh: member: 4 (over y, x), dom: 8 (over z, core).
Axes of the slice: x: 2, y: 2, z: 4, core: 2. Of those that a mesh axis runs over, the one named last changes fastest.
Arguments:
- acoustic_perturbation: float32 [4, 32, 8192], P('member', None, 'dom'), may hold values from -8 to 8
- prior_acoustic_state: float32 [4, 32, 8192], P('member', None, 'dom'), may hold values from -8 to 8
- thermal_anomaly: float32 [4, 32, 8192], P('member', None, 'dom'), may hold values from -8 to 8
- model_parameters: float32 [4, 4], P('member'), may hold values from 0.5 to 1.5
- crossing_velocity: float32 [32, 24576], P(None, 'dom'), may hold values from -3 to 3
- face_extent: float32 [24576], P('dom'), may hold values from 0.1 to 0.4
- face_metric_factor: float32 [24576], P('dom'), may hold values from 0.01 to 0.06
- reciprocal_polygon_surface: float32 [8192], P('dom'), may hold values from 0.5 to 2
- owned_totals: int32 [8], P('dom'), may hold values from 768 to 1024, as said below
- export_lists: int32 [8, 6, 128], P('dom'), may hold values from 0 to 1024, as said below
- face_neighbour_pair: int32 [2, 24576], P(None, 'dom'), may hold values from 0 to 1792, as said below
- polygon_side_lookup: int32 [6, 8192], P(None, 'dom'), may hold values from 0 to 3072, as said below
Outputs:
- pressure_out: float32 [4, 32, 8192], P('member', None, 'dom')
- temperature_out: float32 [4, 32, 8192], P('member', None, 'dom')
- ensemble_mean: float32 [32, 8192], P(None, 'dom')
Inputs may be any that keep to these rules, and one draw needn't show every extreme that they name: The first owned_totals[p] cell slots of partition p are its cells, the rest unused; some partition has 1024. Row export_lists[p, b] lists owned cells of partition p sent to partition (p + offsets[b]) mod 8; filled entries first, then 1024 in the empty slots; at least 64 filled entries a row; in every draw some partition receives 128 filled entries in all 6 of its rows. `face_neighbour_pair`: edge 3 i + j of partition p starts at owned cell i and ends at another owned cell or at halo column 1024 + b * 128 + k whose slot k is filled in the sender's row b; edges of unused cells have both ends at 1792. `polygon_side_lookup`: the local edges with an end at each owned cell, 3072 in empty slots; unused cells have only empty slots.
All inputs are finite; a program needn't handle non-finite values.
Results may differ from a plain program's by a relative error of at most 0.0001.
Values sent between devices are 32-bit elements; how exact they have to be, the bound alone decides.
A program may use at most 64 MiB of HBM per device.

v0:
```python
import functools

import jax
import jax.numpy as jnp
from jax import lax
from jax.experimental import pallas as pl
from jax.experimental.pallas import tpu as pltpu
from jax.sharding import PartitionSpec as P

STEPS = 2
NS = 3
TIME_STEP = 0.25
LANES = 128
MESH = pl.DeviceIdType.MESH
F32 = jnp.float32
BF16 = jnp.bfloat16


def neighbour_offsets(count):
    return [(b // 2 + 1) * (1 - 2 * (b % 2)) for b in range(count)]


def mm(a, b):
    return jnp.dot(a, b, preferred_element_type=F32)


def mm_nt(a, b):
    return lax.dot_general(a, b, (((1,), (1,)), ((), ())), preferred_element_type=F32)


def halves(x):
    high = x.astype(BF16)
    low = (x - high.astype(F32)).astype(BF16)
    return jnp.concatenate([high, low], axis=0)


def fold(x):
    rows = x.shape[0] // 2
    return x[:rows] + x[rows:]


def kernel(
    n,
    members,
    p_ref,
    q_ref,
    t_ref,
    par_ref,
    v_ref,
    ext_ref,
    met_ref,
    inv_ref,
    own_ref,
    exp_ref,
    fin_ref,
    p_out,
    t_out,
    e_out,
    pick,
    g,
    a_hi,
    a_lo,
    b_loc,
    diag,
    xv,
    vj,
    ej,
    send,
    recv,
    mean_send,
    mean_recv,
    mem_send,
    mem_recv,
    mm_send,
    mm_recv,
    send_sem,
    recv_sem,
    mean_ssem,
    mean_rsem,
    mem_ssem,
    mem_rsem,
    mm_ssem,
    mm_rsem,
):
    levels, cells = p_ref.shape[1], p_ref.shape[2]
    slabs = v_ref.shape[1] // cells
    blocks = cells // LANES
    wide = slabs * LANES
    nb = exp_ref.shape[1]
    hb = exp_ref.shape[2]
    halo = nb * hb
    me = lax.axis_index("dom")
    mine = lax.axis_index("member")
    offsets = neighbour_offsets(nb)
    stages = members.bit_length() - 1

    def dom_peer(k):
        return {"dom": lax.rem(me + (k % n), n)}

    def member_peer(stage):
        bit = 1 << stage
        return {"member": mine + bit - 2 * bit * lax.rem(mine // bit, 2)}

    barrier = pltpu.get_barrier_semaphore()
    for k in range(1, n):
        pl.semaphore_signal(barrier, inc=1, device_id=dom_peer(k), device_id_type=MESH)
    for s in range(stages):
        pl.semaphore_signal(barrier, inc=1, device_id=member_peer(s), device_id_type=MESH)

    speed = par_ref[0, 0]
    kappa = 0.5 * par_ref[0, 1]
    mixing = 0.6 * par_ref[0, 2]
    couple = par_ref[0, 3]
    inverse = inv_ref[...]
    owned = lax.broadcasted_iota(jnp.int32, (1, cells), 1) < own_ref[0]
    area = jnp.where(owned, 1.0 / inverse, 0.0)
    started = []

    strip = 16
    sub = lax.broadcasted_iota(jnp.int32, (strip, 1), 0)
    for b in range(nb):
        row = exp_ref[0, b : b + 1, :]

        def build_pick(s, carry, row=row, b=b):
            rows = lax.broadcasted_iota(jnp.int32, (strip, hb), 0) + s * strip
            pick[pl.ds(pl.multiple_of(s * strip, strip), strip), b * hb : (b + 1) * hb] = (
                jnp.where(rows == row, 1.0, 0.0).astype(BF16)
            )
            return carry

        lax.fori_loop(0, cells // strip, build_pick, 0)

    def exchange(slot, chosen):
        copies = []
        for b, offset in enumerate(offsets):
            send[slot, b] = chosen[:, b * hb : (b + 1) * hb]
            copy = pltpu.make_async_remote_copy(
                src_ref=send.at[slot, b],
                dst_ref=recv.at[slot, b],
                send_sem=send_sem.at[slot, b],
                recv_sem=recv_sem.at[slot, b],
                device_id=dom_peer(offset),
                device_id_type=MESH,
            )
            copy.start()
            copies.append(copy)
        started.extend(copies)
        return copies

    def arrived(slot, copies):
        for copy in copies:
            copy.wait_recv()
        return halves(jnp.concatenate([recv[slot, b] for b in range(nb)], axis=1))

    current = p_ref[0]
    previous = q_ref[0]
    theta = t_ref[0]
    xp = halves(current)
    xt = halves(theta)
    both = mm(jnp.concatenate([xt, xp], axis=0), pick[...])
    pl.semaphore_wait(barrier, n - 1 + stages)
    t_copies = exchange(0, fold(both[: 2 * levels]))
    p_copies = exchange(1, fold(both[2 * levels :]))

    base = levels * blocks
    for b in range(blocks):
        cut = slice(b * wide, (b + 1) * wide)
        xv[b * levels : (b + 1) * levels, :] = v_ref[:, cut]
        ends = fin_ref[1:2, cut]
        xv[base + b : base + b + 1, :] = ext_ref[:, cut]
        xv[base + blocks + b : base + blocks + b + 1, :] = met_ref[:, cut]
        xv[base + 2 * blocks + b : base + 2 * blocks + b + 1, :] = (ends // 8).astype(F32)
        xv[base + 3 * blocks + b : base + 3 * blocks + b + 1, :] = (ends % 8).astype(F32)
    ri = lax.broadcasted_iota(jnp.int32, (wide, wide), 0)
    ci = lax.broadcasted_iota(jnp.int32, (wide, wide), 1)
    order = jnp.where(ri == slabs * (ci % LANES) + ci // LANES, 1.0, 0.0).astype(BF16)
    for b in range(blocks):
        y = fold(mm(halves(xv[b * levels : (b + 1) * levels, :]), order))
        for j in range(slabs):
            vj[j, :, b * LANES : (b + 1) * LANES] = y[:, j * LANES : (j + 1) * LANES]
    y = fold(mm(halves(xv[base : base + 4 * blocks, :]), order))
    for kind in range(4):
        for j in range(slabs):
            for b in range(blocks):
                ej[kind * slabs + j : kind * slabs + j + 1, b * LANES : (b + 1) * LANES] = y[
                    kind * blocks + b : kind * blocks + b + 1, j * LANES : (j + 1) * LANES
                ]
    extent = [ej[j : j + 1, :] for j in range(slabs)]
    metric = [ej[slabs + j : slabs + j + 1, :] for j in range(slabs)]
    ends = [
        8.0 * ej[2 * slabs + j : 2 * slabs + j + 1, :] + ej[3 * slabs + j : 3 * slabs + j + 1, :]
        for j in range(slabs)
    ]

    def strip_of(s):
        at = pl.ds(pl.multiple_of(s * strip, strip), strip)
        rows = (lax.broadcasted_iota(jnp.int32, (strip, cells), 0) + s * strip).astype(F32)
        total = jnp.zeros((strip, cells), F32)
        for j in range(slabs):
            hit = rows == ends[j]
            g[at, j * cells : (j + 1) * cells] = jnp.where(hit, 1.0, 0.0).astype(BF16)
            total = total + jnp.where(hit, metric[j], 0.0)
        return at, total

    def put(at, value, columns):
        high = value.astype(BF16)
        a_hi[at, columns] = high
        a_lo[at, columns] = (value - high.astype(F32)).astype(BF16)

    def build_local(s, carry):
        at, total = strip_of(s)
        b_loc[at, :] = total
        return carry

    def build_halo(s, carry):
        at, total = strip_of(s)
        put(at, total, slice(None))
        diag[...] += total
        return carry

    diag[...] = jnp.zeros_like(diag)
    lax.fori_loop(0, cells // strip, build_local, 0)
    lax.fori_loop(cells // strip, (cells + halo) // strip, build_halo, 0)

    def symmetric(i, carry):
        at = pl.ds(pl.multiple_of(i * LANES, LANES), LANES)
        for j in range(blocks):
            cut = slice(j * LANES, (j + 1) * LANES)
            value = b_loc[at, cut] + b_loc[cut, at].T
            put(at, value, cut)
            total = value[:strip]
            for r in range(1, LANES // strip):
                total = total + value[r * strip : (r + 1) * strip]
            diag[:, cut] += total
        return carry

    lax.fori_loop(0, blocks, symmetric, 0)
    degree = jnp.sum(diag[...], axis=0, keepdims=True)
    scale = speed * inverse

    def far_local(x, j):
        return fold(mm(x, g[:cells, j * cells : (j + 1) * cells]))

    def far_halo(x, j):
        return fold(mm(x, g[cells:, j * cells : (j + 1) * cells]))

    def slab_flux(theta, far, j):
        wind = vj[j]
        flux = extent[j] * (
            0.5 * wind * (theta + far) - (0.5 * jnp.abs(wind) + kappa) * (far - theta)
        )
        incoming = mm_nt(halves(flux), g[:cells, j * cells : (j + 1) * cells])
        return flux - fold(incoming)

    def theta_end(theta, div):
        step = theta[1:] - theta[:-1]
        zero = jnp.zeros((1, cells), F32)
        vertical = mixing * (
            jnp.concatenate([step, zero], 0) - jnp.concatenate([zero, step], 0)
        )
        advanced = jnp.where(owned, theta + TIME_STEP * (vertical - inverse * div), theta)
        return advanced, couple * (advanced - theta) / NS

    def local_part(x):
        return fold(mm(x, a_hi[:cells, :])) + mm(x[:levels], a_lo[:cells, :])

    def halo_part(x):
        return fold(mm(x, a_hi[cells:, :])) + mm(x[:levels], a_lo[cells:, :])

    def partial_mean(slot, field):
        weighted = jnp.sum(field * area, axis=1, keepdims=True)
        whole = jnp.sum(area, axis=1, keepdims=True)
        row_at = lax.broadcasted_iota(jnp.int32, (levels, LANES), 0)
        lane_at = lax.broadcasted_iota(jnp.int32, (levels, LANES), 1)
        row = jnp.sum(jnp.where(row_at == lane_at, weighted, 0.0), axis=0, keepdims=True)
        lane = lax.broadcasted_iota(jnp.int32, (1, LANES), 1)
        row = jnp.where(lane < levels, row, whole)
        mean_send[slot] = jnp.broadcast_to(row, (8, LANES))
        copies = []
        for k in range(1, n):
            copy = pltpu.make_async_remote_copy(
                src_ref=mean_send.at[slot],
                dst_ref=mean_recv.at[slot, k - 1],
                send_sem=mean_ssem.at[slot, k - 1],
                recv_sem=mean_rsem.at[slot, k - 1],
                device_id=dom_peer(k),
                device_id_type=MESH,
            )
            copy.start()
            copies.append(copy)
        started.extend(copies)
        return copies

    def mean_row(slot, copies):
        total = mean_send[slot]
        for k, copy in enumerate(copies):
            copy.wait_recv()
            total = total + mean_recv[slot, k]
        return total / total[:, levels : levels + 1]

    def as_column(row):
        row_at = lax.broadcasted_iota(jnp.int32, (levels, LANES), 0)
        lane_at = lax.broadcasted_iota(jnp.int32, (levels, LANES), 1)
        return jnp.sum(jnp.where(row_at == lane_at, row[0:1], 0.0), axis=1, keepdims=True)

    ht = arrived(0, t_copies)
    div = jnp.zeros((levels, cells), F32)
    for j in range(slabs):
        div = div + slab_flux(theta, far_local(xt, j) + far_halo(ht, j), j)
    theta1, forcing = theta_end(theta, div)
    xt1 = halves(theta1)

    mean_copies = None
    slot = 1
    total_substeps = STEPS * NS
    div = jnp.zeros((levels, cells), F32)
    ht1 = None
    for k in range(total_substeps):
        accel = local_part(xp) - degree * current
        if k == NS - 1:
            ht1 = arrived(0 + STEPS * NS + 1, t_copies)
            for j in range(slabs - 1):
                div = div + slab_flux(theta1, far_local(xt1, j) + far_halo(ht1, j), j)
        if k == NS:
            mean_copies = partial_mean(0, current)
            j = slabs - 1
            div = div + slab_flux(theta1, far_local(xt1, j) + far_halo(ht1, j), j)
            theta2, forcing = theta_end(theta1, div)
            t_out[0] = theta2
        accel = accel + halo_part(arrived(slot, p_copies))
        stepped = jnp.where(
            owned, 2.0 * current - previous + scale * accel + forcing, current
        )
        previous, current = current, stepped
        if k < total_substeps - 1:
            slot += 1
            xp = halves(current)
            p_copies = exchange(slot, fold(mm(xp, pick[...])))
            if k == 0:
                t_copies = exchange(STEPS * NS + 1, fold(mm(xt1, pick[...])))

    first = as_column(mean_row(0, mean_copies))
    current = jnp.where(owned, current - first, current)

    width = cells // max(stages, 1)
    last_copies = partial_mean(1, current)
    e_out[...] = current

    def member_stage(stage):
        copies = []
        for c in range(stages):
            cut = slice(c * width, (c + 1) * width)
            mem_send[stage, c] = e_out[:, cut]
            copy = pltpu.make_async_remote_copy(
                src_ref=mem_send.at[stage, c],
                dst_ref=mem_recv.at[stage, c],
                send_sem=mem_ssem.at[stage, c],
                recv_sem=mem_rsem.at[stage, c],
                device_id=member_peer((stage + c) % stages),
                device_id_type=MESH,
            )
            copy.start()
            copies.append(copy)
        started.extend(copies)
        return copies

    def member_add(stage, copies):
        for c, copy in enumerate(copies):
            cut = slice(c * width, (c + 1) * width)
            copy.wait_recv()
            e_out[:, cut] = mem_send[stage, c] + mem_recv[stage, c]

    bulk = member_stage(0) if stages else []
    last = mean_row(1, last_copies)
    summed = last
    p_out[0] = jnp.where(owned, current - as_column(last), current)
    for s in range(stages):
        mm_send[s] = summed
        copy = pltpu.make_async_remote_copy(
            src_ref=mm_send.at[s],
            dst_ref=mm_recv.at[s],
            send_sem=mm_ssem.at[s],
            recv_sem=mm_rsem.at[s],
            device_id=member_peer(s),
            device_id_type=MESH,
        )
        copy.start()
        started.append(copy)
        member_add(s, bulk)
        if s + 1 < stages:
            bulk = member_stage(s + 1)
        copy.wait_recv()
        summed = mm_send[s] + mm_recv[s]
    e_out[...] = (e_out[...] - jnp.where(owned, as_column(summed), 0.0)) / members
    for copy in started:
        copy.wait_send()


def solution(mesh):
    n = mesh.shape["dom"]
    members = mesh.shape["member"]

    def per_device(
        acoustic_perturbation,
        prior_acoustic_state,
        thermal_anomaly,
        model_parameters,
        crossing_velocity,
        face_extent,
        face_metric_factor,
        reciprocal_polygon_surface,
        owned_totals,
        export_lists,
        face_neighbour_pair,
        polygon_side_lookup,
    ):
        _, levels, cells = acoustic_perturbation.shape
        edges = face_extent.shape[0]
        slabs = edges // cells
        blocks = cells // LANES
        nb, hb = export_lists.shape[1:]
        halo = nb * hb
        stages = members.bit_length() - 1
        some = max(stages, 1)
        slots = STEPS * NS + 2
        vmem = pl.BlockSpec(memory_space=pltpu.VMEM)
        smem = pl.BlockSpec(memory_space=pltpu.SMEM)
        dma = pltpu.SemaphoreType.DMA
        return pl.pallas_call(
            functools.partial(kernel, n, members),
            out_shape=(
                jax.ShapeDtypeStruct((1, levels, cells), F32),
                jax.ShapeDtypeStruct((1, levels, cells), F32),
                jax.ShapeDtypeStruct((levels, cells), F32),
            ),
            in_specs=[vmem, vmem, vmem, smem, vmem, vmem, vmem, vmem, smem, vmem, vmem],
            out_specs=(vmem, vmem, vmem),
            scratch_shapes=[
                pltpu.VMEM((cells, halo), BF16),
                pltpu.VMEM((cells + halo, edges), BF16),
                pltpu.VMEM((cells + halo, cells), BF16),
                pltpu.VMEM((cells + halo, cells), BF16),
                pltpu.VMEM((cells, cells), F32),
                pltpu.VMEM((16, cells), F32),
                pltpu.VMEM((levels * blocks + 4 * blocks, slabs * LANES), F32),
                pltpu.VMEM((slabs, levels, cells), F32),
                pltpu.VMEM((16, cells), F32),
                pltpu.VMEM((slots, nb, levels, hb), F32),
                pltpu.VMEM((slots, nb, levels, hb), F32),
                pltpu.VMEM((STEPS, 8, LANES), F32),
                pltpu.VMEM((STEPS, n - 1, 8, LANES), F32),
                pltpu.VMEM((some, some, levels, cells // some), F32),
                pltpu.VMEM((some, some, levels, cells // some), F32),
                pltpu.VMEM((some, 8, LANES), F32),
                pltpu.VMEM((some, 8, LANES), F32),
                dma((slots, nb)),
                dma((slots, nb)),
                dma((STEPS, n - 1)),
                dma((STEPS, n - 1)),
                dma((some, some)),
                dma((some, some)),
                dma((some,)),
                dma((some,)),
            ],
            compiler_params=pltpu.CompilerParams(
                collective_id=0, has_side_effects=True, vmem_limit_bytes=60 * 1024 * 1024
            ),
        )(
            acoustic_perturbation,
            prior_acoustic_state,
            thermal_anomaly,
            model_parameters,
            crossing_velocity,
            face_extent[None],
            face_metric_factor[None],
            reciprocal_polygon_surface[None],
            owned_totals,
            export_lists,
            face_neighbour_pair,
        )

    in_specs = (
        P("member", None, "dom"),
        P("member", None, "dom"),
        P("member", None, "dom"),
        P("member", None),
        P(None, "dom"),
        P("dom"),
        P("dom"),
        P("dom"),
        P("dom"),
        P("dom", None, None),
        P(None, "dom"),
        P(None, "dom"),
    )
    out_specs = (P("member", None, "dom"), P("member", None, "dom"), P(None, "dom"))
    return jax.shard_map(
        per_device, mesh=mesh, in_specs=in_specs, out_specs=out_specs, check_vma=False
    )
```

profile of v0, /device:TPU:0, one launch (start us, length us, event | category | flops | bytes accessed | tf_op | source)
XLA Modules:
  0.0 63.5 jit_solution(1622990878739127110)
XLA Ops:
  1.3 0.0 copy-start.2
  1.3 0.7 %copy-done.2 = s32[1,6,128]{2,0,1:T(1,128)S(1)} copy-done((s32[1,6,128]{2,0,1:T(1,128)S(1)}, s32[1,6,128]{2,0,1:T(1,128)}, u32[]{:S(2)}) %copy-start.2) | copy-done | bytes 3096
  2.0 0.6 copy.14.exp_ref
  2.6 57.7 %shard_map.130 = (f32[1,32,1024]{2,1,0:T(8,128)}, f32[1,32,1024]{2,1,0:T(8,128)}, f32[32,1024]{1,0:T(8,128)}) custom-call(f32[1,32,1024]{2,1,0:T(8,128)} %p_ref.1, f32[1,32,1024]{2,1,0:T(8,128)} %q_ref.1, f32[1,32,1024]{2,1,0:T(8,128)} %t_ref.1, f32[1,4]{1,0:T(1,128)} %par_ref.1, f32[32,3072]{1,0:T(8,128)} %v_ref.1, f32[1,3072]{1,0:T(1,128)} %bitcast.3, ...), custom_call_target="tpu_custom_call" | custom-call | tf_op jit(solution)/shard_map/pallas_call | solution.py:429
  60.2 0.0 copy-start.1
  60.2 1.6 %copy.19 = f32[1,32,1024]{2,1,0:T(8,128)} copy(f32[1,32,1024]{2,1,0:T(8,128)} %get-tuple-element.6) | data formatting | bytes 262144
  61.8 0.0 copy-done.1
  61.8 0.0 copy-start
  61.8 0.7 %copy.20 = f32[1,32,1024]{2,1,0:T(8,128)} copy(f32[1,32,1024]{2,1,0:T(8,128)S(1)} %copy-done.1) | data formatting | bytes 262144
  62.5 0.3 copy-done
  62.8 0.7 %copy.21 = f32[32,1024]{1,0:T(8,128)} copy(f32[32,1024]{1,0:T(8,128)S(1)} %copy-done) | data formatting | bytes 262144
Async XLA Ops:
  1.3 0.7 %copy-start.2 = (s32[1,6,128]{2,0,1:T(1,128)S(1)}, s32[1,6,128]{2,0,1:T(1,128)}, u32[]{:S(2)}) copy-start(s32[1,6,128]{2,0,1:T(1,128)} %param.21) | copy-start | bytes 9220
  60.2 1.6 %copy-start.1 = (f32[1,32,1024]{2,1,0:T(8,128)S(1)}, f32[1,32,1024]{2,1,0:T(8,128)}, u32[]{:S(2)}) copy-start(f32[1,32,1024]{2,1,0:T(8,128)} %get-tuple-element.7) | copy-start | bytes 393220
  61.8 1.0 %copy-start = (f32[32,1024]{1,0:T(8,128)S(1)}, f32[32,1024]{1,0:T(8,128)}, u32[]{:S(2)}) copy-start(f32[32,1024]{1,0:T(8,128)} %get-tuple-element.8) | copy-start | bytes 393220
where the time goes:
time: 63.7 us; the launch traced here: 63.5 us
  Pallas kernels  57.7 us (91%)
  local copies, waits for them, and re-layouts  4.48 us (7%)
  between operations  1.3 us (2%)
    pallas_call x1, Pallas kernels, per_device(): pl.pallas_call(functools.partial(kernel, n, members), out_shape=(jax.Shap...  57.7 us
    unnamed x10, local copies, waits for them, and re-layouts  4.48 us

commit v1 on v0

v1 whole, which is shorter than its diff:
```python
import functools

import jax
import jax.numpy as jnp
from jax import lax
from jax.experimental import pallas as pl
from jax.experimental.pallas import tpu as pltpu
from jax.sharding import PartitionSpec as P

STEPS = 2
NS = 3
TIME_STEP = 0.25
LANES = 128
CHUNKS = 2
MESH = pl.DeviceIdType.MESH
F32 = jnp.float32
BF16 = jnp.bfloat16
F8 = jnp.float8_e4m3fn
I8 = jnp.int8
scope = jax.named_scope


def neighbour_offsets(count):
    return [(b // 2 + 1) * (1 - 2 * (b % 2)) for b in range(count)]


def mm(a, b):
    return jnp.dot(a, b, preferred_element_type=F32)


def mm_nt(a, b):
    return lax.dot_general(a, b, (((1,), (1,)), ((), ())), preferred_element_type=F32)


def halves(x):
    high = x.astype(BF16)
    low = (x - high.astype(F32)).astype(BF16)
    return jnp.concatenate([high, low], axis=0)


def fold(x):
    rows = x.shape[0] // 2
    return x[:rows] + x[rows:]


def one_hot(dst, row_blocks, columns, row_of):
    width = 512 if columns % 512 == 0 else 256 if columns % 256 == 0 else LANES

    def body(b, carry):
        for at in range(0, columns, width):
            cut = slice(at, at + width)
            row = row_of(cut)
            near = jnp.where((row >> 7) == b, row & (LANES - 1), -1)
            near = jnp.broadcast_to(near, (32, width)).astype(I8)
            for s in range(0, LANES, 32):
                rows = (lax.broadcasted_iota(jnp.int32, (32, width), 0) + s).astype(I8)
                dst[pl.ds(pl.multiple_of(b * LANES + s, 32), 32), cut] = jnp.where(
                    rows == near, F8(1), F8(0)
                )
        return carry

    lax.fori_loop(0, row_blocks, body, 0)


def kernel(
    n,
    members,
    par_hbm,
    p_hbm,
    q_hbm,
    t_hbm,
    v_hbm,
    ext_hbm,
    met_hbm,
    inv_hbm,
    exp_hbm,
    fin_hbm,
    p_hold,
    t_hold,
    e_hold,
    par_ref,
    p_out,
    t_out,
    e_out,
    p_ref,
    q_ref,
    t_ref,
    v_ref,
    ext_ref,
    met_ref,
    inv_ref,
    exp_ref,
    fin_ref,
    in_sem,
    out_sem,
    pick,
    g,
    m3,
    tab,
    itab,
    ej,
    endj,
    ends_s,
    cf,
    ct,
    send,
    recv,
    mean_send,
    mean_recv,
    mem_send,
    mem_recv,
    mm_send,
    mm_recv,
    w_send,
    w_recv,
    send_sem,
    recv_sem,
    mean_ssem,
    mean_rsem,
    mem_ssem,
    mem_rsem,
    mm_sem,
    w_sem,
):
    levels, cells = p_ref.shape[1], p_ref.shape[2]
    slabs = v_ref.shape[1] // cells
    blocks = cells // LANES
    nb, hb = send.shape[1], send.shape[3]
    halo = nb * hb
    me = lax.axis_index("dom")
    mine = lax.axis_index("member")
    offsets = neighbour_offsets(nb)
    stages = members.bit_length() - 1

    def dom_peer(k):
        return {"dom": lax.rem(me + (k % n), n)}

    def member_peer(k):
        return {"member": lax.rem(mine + (k % members), members)}

    def partner(stage):
        bit = 1 << stage
        return {"member": mine + bit - 2 * bit * lax.rem(mine // bit, 2)}

    with scope("start"):
        barrier = pltpu.get_barrier_semaphore()
        for k in range(1, n):
            pl.semaphore_signal(barrier, inc=1, device_id=dom_peer(k), device_id_type=MESH)
        for k in range(1, members):
            pl.semaphore_signal(barrier, inc=1, device_id=member_peer(k), device_id_type=MESH)
        loads = {}
        for at, (name, src, dst) in enumerate(
            [
                ("exp", exp_hbm, exp_ref),
                ("t", t_hbm, t_ref),
                ("p", p_hbm, p_ref),
                ("fin", fin_hbm, fin_ref),
                ("par", par_hbm, par_ref),
                ("met", met_hbm, met_ref),
                ("inv", inv_hbm, inv_ref),
                ("ext", ext_hbm, ext_ref),
                ("v", v_hbm, v_ref),
                ("q", q_hbm, q_ref),
            ]
        ):
            loads[name] = pltpu.make_async_copy(src, dst, in_sem.at[at])
            loads[name].start()


    def to_peer(src, dst, send_sem, recv_sem, peer):
        return pltpu.make_async_remote_copy(
            src_ref=src,
            dst_ref=dst,
            send_sem=send_sem,
            recv_sem=recv_sem,
            device_id=peer,
            device_id_type=MESH,
        )

    def exchange(slot, chosen):
        for b, offset in enumerate(offsets):
            send[slot, b] = chosen[:, b * hb : (b + 1) * hb]
            to_peer(
                send.at[slot, b],
                recv.at[slot, b],
                send_sem.at[0],
                recv_sem.at[slot],
                dom_peer(offset),
            ).start()

    def arrived(slot):
        to_peer(
            send.at[slot], recv.at[slot], send_sem.at[0], recv_sem.at[slot], dom_peer(1)
        ).wait_recv()
        return halves(jnp.concatenate([recv[slot, b] for b in range(nb)], axis=1))

    def chosen_of(*fields):
        y = mm(jnp.concatenate([halves(x) for x in fields], axis=0), pick[...])
        return [fold(y[2 * levels * i : 2 * levels * (i + 1)]) for i in range(len(fields))]

    with scope("pick_build"):
        loads["exp"].wait()
        one_hot(pick, blocks, halo, lambda cut: exp_ref[0:1, cut])
    with scope("pick0"):
        loads["t"].wait()
        loads["p"].wait()
        current = p_ref[0]
        theta = t_ref[0]
        theta_s, current_s = chosen_of(theta, current)

    with scope("tables"):
        loads["fin"].wait()
        loads["met"].wait()
        loads["inv"].wait()
        loads["ext"].wait()
        loads["par"].wait()
        speed = par_ref[0, 0]
        kappa = 0.5 * par_ref[0, 1]
        mixing = 0.6 * par_ref[0, 2]
        couple = par_ref[0, 3]
        tab[0:8, :] = jnp.broadcast_to(met_ref[...], (8, slabs * cells))
        tab[8:16, :] = jnp.broadcast_to(ext_ref[...], (8, slabs * cells))
        itab[...] = jnp.broadcast_to(fin_ref[1:2, :], (8, slabs * cells))

        def slab(ref, rows, b, j):
            at = slabs * lax.broadcasted_iota(jnp.int32, (rows, LANES), 1) + j
            block, lane = at >> 7, at & (LANES - 1)
            out = None
            for s in range(slabs):
                lo = (slabs * b + s) * LANES
                y = jnp.take_along_axis(
                    ref[0:rows, lo : lo + LANES], lane, axis=1, mode="promise_in_bounds"
                )
                out = y if out is None else jnp.where(block == s, y, out)
            return out

        for b in range(blocks):
            for j in range(slabs):
                lo = j * cells + b * LANES
                ej[:, lo : lo + LANES] = slab(tab, 16, b, j)
                endj[:, lo : lo + LANES] = slab(itab, 8, b, j)
        inverse = inv_ref[...]
        owned = endj[0:1, :cells] < cells + halo
        area = jnp.where(owned, 1.0 / inverse, 0.0)
        scale = jnp.where(owned, speed * inverse, 0.0)
        rate = jnp.where(owned, TIME_STEP * inverse, 0.0)
    cuts = [slice(j * cells, (j + 1) * cells) for j in range(slabs)]
    metric = [ej[0:1, cut] for cut in cuts]
    extent = [ej[8:9, cut] for cut in cuts]

    with scope("bar_wait"):
        pl.semaphore_wait(barrier, n - 1 + members - 1)
    with scope("send0"):
        exchange(0, theta_s)
        exchange(1, current_s)

    with scope("g_build"):
        one_hot(g, (cells + halo) // LANES, slabs * cells, lambda cut: endj[0:1, cut])
    with scope("coef"):
        loads["v"].wait()
        for j in range(slabs):
            for b in range(blocks):
                lanes = slice(b * LANES, (b + 1) * LANES)
                wind = slab(v_ref, levels, b, j)
                down = extent[j][:, lanes] * (0.5 * wind - (0.5 * jnp.abs(wind) + kappa))
                cf[j, :, lanes] = down
                ct[j, :, lanes] = extent[j][:, lanes] * wind - down
    with scope("m3_build"):
        rows = [endj[0:1, cut].astype(F32) for cut in cuts] + [scale * m for m in metric]
        rows = jnp.concatenate(rows + [jnp.zeros((16 - 2 * slabs, cells), F32)], axis=0)
        y = fold(mm(halves(rows), pick[...]))
        for j in range(slabs):
            ends_s[0:1, j * halo : (j + 1) * halo] = y[j : j + 1].astype(jnp.int32) - cells
        weight_s = [y[slabs + j : slabs + j + 1] for j in range(slabs)]
        one_hot(m3, nb, slabs * halo, lambda cut: ends_s[0:1, cut])

    def local(pressure, heat=None):
        lhs = [halves(pressure)] + ([] if heat is None else [halves(heat)])
        lhs = jnp.concatenate(lhs, axis=0)
        p_flux, t_flux = [], []
        for j in range(slabs):
            y = mm(lhs, g[:cells, cuts[j]])
            p_flux.append(metric[j] * (fold(y[: 2 * levels]) - pressure))
            if heat is not None:
                t_flux.append(cf[j] * fold(y[2 * levels :]) + ct[j] * heat)
        lhs = [halves(jnp.concatenate(p_flux, axis=1))]
        if heat is not None:
            lhs.append(halves(jnp.concatenate(t_flux, axis=1)))
        y = mm_nt(jnp.concatenate(lhs, axis=0), g[:cells, :])
        p_sum = sum(p_flux[1:], p_flux[0]) - fold(y[: 2 * levels])
        if heat is None:
            return p_sum
        return p_sum, sum(t_flux[1:], t_flux[0]) - fold(y[2 * levels :])

    def far(x, j):
        return mm(x, g[cells:, cuts[j]])

    def far_s(x, j):
        return mm(x, m3[:, j * halo : (j + 1) * halo])

    def heat_base(heat, div):
        step = heat[1:] - heat[:-1]
        zero = jnp.zeros((1, cells), F32)
        vertical = mixing * (
            jnp.concatenate([step, zero], 0) - jnp.concatenate([zero, step], 0)
        )
        return heat + jnp.where(owned, TIME_STEP * vertical, 0.0) - rate * div

    def lane_blocks(x):
        parts = [x[:, b * LANES : (b + 1) * LANES] for b in range(x.shape[1] // LANES)]
        return sum(parts[1:], parts[0])

    def partial_mean(slot, weighted):
        weighted = jnp.sum(weighted, axis=1, keepdims=True)
        whole = jnp.sum(area, axis=1, keepdims=True)
        row_at = lax.broadcasted_iota(jnp.int32, (levels, LANES), 0)
        lane_at = lax.broadcasted_iota(jnp.int32, (levels, LANES), 1)
        row = jnp.sum(jnp.where(row_at == lane_at, weighted, 0.0), axis=0, keepdims=True)
        lane = lax.broadcasted_iota(jnp.int32, (1, LANES), 1)
        row = jnp.where(lane < levels, row, whole)
        mean_send[slot] = jnp.broadcast_to(row, (8, LANES))
        for k in range(1, n):
            to_peer(
                mean_send.at[slot],
                mean_recv.at[slot, k - 1],
                mean_ssem.at[0],
                mean_rsem.at[slot],
                dom_peer(k),
            ).start()

    def mean_row(slot):
        to_peer(
            mean_recv.at[slot],
            mean_recv.at[slot],
            mean_ssem.at[0],
            mean_rsem.at[slot],
            dom_peer(1),
        ).wait_recv()
        total = mean_send[slot]
        for k in range(n - 1):
            total = total + mean_recv[slot, k]
        return total / total[:, levels : levels + 1]

    def as_column(row):
        row_at = lax.broadcasted_iota(jnp.int32, (levels, LANES), 0)
        lane_at = lax.broadcasted_iota(jnp.int32, (levels, LANES), 1)
        return jnp.sum(jnp.where(row_at == lane_at, row[0:1], 0.0), axis=1, keepdims=True)

    with scope("local_0"):
        p_sum, t_sum = local(current, theta)
        loads["q"].wait()
        base = jnp.where(owned, 2.0 * current - q_ref[0], current) + scale * p_sum
        t_base = heat_base(theta, t_sum)
    with scope("base_0"):
        base_s, t_base_s, *turn_s = chosen_of(
            base, t_base, *[rate * cf[j] for j in range(slabs)]
        )
    with scope("wait_0"):
        ht = arrived(0)
        hp = arrived(1)
    share = couple / NS
    with scope("crit_0"):
        both = jnp.concatenate([ht, hp], axis=0)
        out, t_out_s = base_s, t_base_s
        for j in range(slabs):
            y = far_s(both, j)
            t_out_s = t_out_s - turn_s[j] * fold(y[: 2 * levels])
            out = out + weight_s[j] * fold(y[2 * levels :])
        out = out + share * (t_out_s - theta_s)
        exchange(2, out)
        exchange(STEPS * NS + 1, t_out_s)
    with scope("full_0"):
        theta1 = t_base
        previous, stepped = current, base
        for j in range(slabs):
            y = far(both, j)
            theta1 = theta1 - rate * (cf[j] * fold(y[: 2 * levels]))
            stepped = stepped + (scale * metric[j]) * fold(y[2 * levels :])
        forcing = share * (theta1 - theta)
        current = stepped + forcing

    def w_copy(b, offset):
        whole = offset == 0
        return to_peer(
            w_send if whole else w_send.at[b],
            w_recv if whole else w_recv.at[b],
            w_sem.at[0],
            w_sem.at[1],
            dom_peer(1 if whole else offset),
        )

    total = STEPS * NS
    for k in range(1, total):
        with scope(f"local_{k}"):
            if k == 1:
                p_sum, t_sum = local(current, theta1)
                t_base = heat_base(theta1, t_sum)
            else:
                p_sum = local(current)
            if k == NS - 1:
                ht = arrived(STEPS * NS + 1)
                theta2 = t_base
                for j in range(slabs):
                    theta2 = theta2 - rate * (cf[j] * fold(far(ht, j)))
                t_out[0] = theta2
                t_copy = pltpu.make_async_copy(t_out, t_hold, out_sem.at[0])
                t_copy.start()
            if k == NS:
                forcing = share * (theta2 - theta1)
                partial_mean(0, lane_blocks(current * area))
            base = (
                jnp.where(owned, 2.0 * current - previous, current) + scale * p_sum + forcing
            )
        if k < total - 1:
            with scope(f"base_{k}"):
                (base_s,) = chosen_of(base)
        else:
            with scope("mean_1"):
                w_copy(0, 0).wait_recv()
                weighted = lane_blocks(base * area)
                for b in range(nb):
                    weighted = weighted + w_recv[b, 0:1] * send[k + 1, b]
                partial_mean(1, weighted)
                first_row = mean_row(0)
                first = as_column(first_row)
        if k == NS:
            with scope("pull"):
                rows = jnp.concatenate(
                    [speed * m for m in metric], axis=1
                )
                rows = halves(jnp.broadcast_to(rows, (16, slabs * cells)))
                w = fold(mm_nt(rows, g[cells:, :]))
                for b, offset in enumerate(offsets):
                    w_send[b] = w[0:8, b * hb : (b + 1) * hb]
                    w_copy(b, -offset).start()
        with scope(f"wait_{k}"):
            hp = arrived(k + 1)
        if k < total - 1:
            with scope(f"crit_{k}"):
                out = base_s
                for j in range(slabs):
                    out = out + weight_s[j] * fold(far_s(hp, j))
                exchange(k + 2, out)
        with scope(f"full_{k}"):
            previous, stepped = current, base
            for j in range(slabs):
                stepped = stepped + (scale * metric[j]) * fold(far(hp, j))
            current = stepped

    with scope("tail_send"):
        current = jnp.where(owned, current - first, current)
        pieces = max(stages, 1) * CHUNKS
        width = cells // pieces

        def member_copy(stage, c):
            return to_peer(
                mem_send.at[stage, c],
                mem_recv.at[stage, c],
                mem_ssem.at[0],
                mem_rsem.at[stage, c],
                partner((stage + c) % max(stages, 1)),
            )

        def row_copy(k):
            return to_peer(
                mm_send, mm_recv.at[k - 1], mm_sem.at[0], mm_sem.at[1], member_peer(k)
            )

        for c in range(pieces):
            mem_send[0, c] = current[:, c * width : (c + 1) * width]
            if stages:
                member_copy(0, c).start()
    with scope("tail_mean"):
        last = mean_row(1) - first_row
        mm_send[...] = last
        for k in range(1, members):
            row_copy(k).start()
        column = as_column(last)
        p_out[0] = jnp.where(owned, current - column, current)
        p_copy = pltpu.make_async_copy(p_out, p_hold, out_sem.at[1])
        p_copy.start()
    for s in range(stages - 1):
        with scope(f"tail_stage_{s}"):
            for c in range(pieces):
                member_copy(s, c).wait_recv()
                mem_send[s + 1, c] = mem_send[s, c] + mem_recv[s, c]
                member_copy(s + 1, c).start()
    with scope("tail_rows"):
        summed = last
        if members > 1:
            to_peer(mm_recv, mm_recv, mm_sem.at[0], mm_sem.at[1], member_peer(1)).wait_recv()
            for k in range(members - 1):
                summed = summed + mm_recv[k]
        column = as_column(summed)
    with scope("tail_end"):
        for c in range(pieces):
            cut = slice(c * width, (c + 1) * width)
            field = mem_send[max(stages - 1, 0), c]
            if stages:
                member_copy(stages - 1, c).wait_recv()
                field = field + mem_recv[stages - 1, c]
            e_out[:, cut] = (field - jnp.where(owned[:, cut], column, 0.0)) / members
        e_copy = pltpu.make_async_copy(e_out, e_hold, out_sem.at[2])
        e_copy.start()
    with scope("drain"):
        to_peer(send, recv, send_sem.at[0], recv_sem.at[0], dom_peer(1)).wait_send()
        to_peer(mean_recv, mean_recv, mean_ssem.at[0], mean_rsem.at[0], dom_peer(1)).wait_send()
        w_copy(0, 0).wait_send()
        if stages:
            to_peer(
                mem_send, mem_recv, mem_ssem.at[0], mem_rsem.at[0, 0], partner(0)
            ).wait_send()
        if members > 1:
            to_peer(mm_recv, mm_recv, mm_sem.at[0], mm_sem.at[1], member_peer(1)).wait_send()
        t_copy.wait()
        p_copy.wait()
        e_copy.wait()


def finish(p_hold, t_hold, e_hold, p_out, t_out, e_out, sem):
    copies = [
        pltpu.make_async_copy(src, dst, sem.at[at])
        for at, (src, dst) in enumerate(
            [(p_hold, p_out), (t_hold, t_out), (e_hold, e_out)]
        )
    ]
    for copy in copies:
        copy.start()
    for copy in copies:
        copy.wait()


def solution(mesh):
    n = mesh.shape["dom"]
    members = mesh.shape["member"]

    def per_device(
        acoustic_perturbation,
        prior_acoustic_state,
        thermal_anomaly,
        model_parameters,
        crossing_velocity,
        face_extent,
        face_metric_factor,
        reciprocal_polygon_surface,
        owned_totals,
        export_lists,
        face_neighbour_pair,
        polygon_side_lookup,
    ):
        _, levels, cells = acoustic_perturbation.shape
        edges = face_extent.shape[0]
        slabs = edges // cells
        nb, hb = export_lists.shape[1:]
        halo = nb * hb
        stages = members.bit_length() - 1
        some = max(stages, 1)
        pieces = some * CHUNKS
        slots = STEPS * NS + 2
        hbm = pl.BlockSpec(memory_space=pl.ANY)
        dma = pltpu.SemaphoreType.DMA
        field = pltpu.VMEM((1, levels, cells), F32)
        shapes = (
            jax.ShapeDtypeStruct((1, levels, cells), F32),
            jax.ShapeDtypeStruct((1, levels, cells), F32),
            jax.ShapeDtypeStruct((levels, cells), F32),
        )
        held = pl.pallas_call(
            functools.partial(kernel, n, members),
            out_shape=shapes,
            in_specs=[hbm] * 10,
            out_specs=(hbm, hbm, hbm),
            scratch_shapes=[
                pltpu.SMEM((1, 4), F32),
                field,
                field,
                pltpu.VMEM((levels, cells), F32),
                field,
                field,
                field,
                pltpu.VMEM((levels, edges), F32),
                pltpu.VMEM((1, edges), F32),
                pltpu.VMEM((1, edges), F32),
                pltpu.VMEM((1, cells), F32),
                pltpu.VMEM((1, halo), jnp.int32),
                pltpu.VMEM((2, edges), jnp.int32),
                dma((10,)),
                dma((3,)),
                pltpu.VMEM((cells, halo), F8),
                pltpu.VMEM((cells + halo, edges), F8),
                pltpu.VMEM((halo, slabs * halo), F8),
                pltpu.VMEM((16, edges), F32),
                pltpu.VMEM((8, edges), jnp.int32),
                pltpu.VMEM((16, edges), F32),
                pltpu.VMEM((8, edges), jnp.int32),
                pltpu.VMEM((8, slabs * halo), jnp.int32),
                pltpu.VMEM((slabs, levels, cells), F32),
                pltpu.VMEM((slabs, levels, cells), F32),
                pltpu.VMEM((slots, nb, levels, hb), F32),
                pltpu.VMEM((slots, nb, levels, hb), F32),
                pltpu.VMEM((STEPS, 8, LANES), F32),
                pltpu.VMEM((STEPS, n - 1, 8, LANES), F32),
                pltpu.VMEM((some, pieces, levels, cells // pieces), F32),
                pltpu.VMEM((some, pieces, levels, cells // pieces), F32),
                pltpu.VMEM((8, LANES), F32),
                pltpu.VMEM((max(members - 1, 1), 8, LANES), F32),
                pltpu.VMEM((nb, 8, hb), F32),
                pltpu.VMEM((nb, 8, hb), F32),
                dma((1,)),
                dma((slots,)),
                dma((1,)),
                dma((STEPS,)),
                dma((1,)),
                dma((some, pieces)),
                dma((2,)),
                dma((2,)),
            ],
            compiler_params=pltpu.CompilerParams(
                collective_id=0, has_side_effects=True, vmem_limit_bytes=32 * 1024 * 1024
            ),
        )(
            *[
                pltpu.with_memory_space_constraint(x, pltpu.HBM)
                for x in (
                    model_parameters,
                    acoustic_perturbation,
                    prior_acoustic_state,
                    thermal_anomaly,
                    crossing_velocity,
                    face_extent[None],
                    face_metric_factor[None],
                    reciprocal_polygon_surface[None],
                    export_lists.reshape(1, halo),
                    face_neighbour_pair,
                )
            ],
        )
        return pl.pallas_call(
            finish,
            out_shape=shapes,
            in_specs=[hbm] * 3,
            out_specs=(hbm, hbm, hbm),
            scratch_shapes=[dma((3,))],
            compiler_params=pltpu.CompilerParams(vmem_limit_bytes=1024 * 1024),
        )(*held)

    in_specs = (
        P("member", None, "dom"),
        P("member", None, "dom"),
        P("member", None, "dom"),
        P("member", None),
        P(None, "dom"),
        P("dom"),
        P("dom"),
        P("dom"),
        P("dom"),
        P("dom", None, None),
        P(None, "dom"),
        P(None, "dom"),
    )
    out_specs = (P("member", None, "dom"), P("member", None, "dom"), P(None, "dom"))
    return jax.shard_map(
        per_device, mesh=mesh, in_specs=in_specs, out_specs=out_specs, check_vma=False
    )
```

time: 63.7 us -> 45 us (0.71)
  Pallas kernels: 57.7 us -> 44.1 us
  local copies, waits for them, and re-layouts: 4.48 us -> 0 us
    pallas_call x1 -> x2, Pallas kernels: 57.7 us -> 44.1 us  [the longest x1 43.3 us: per_device(): pl.pallas_call(functools.partial(kernel, n, members), out_shape=shapes, i...]
    unnamed x10 -> x0, local copies, waits for them, and re-layouts: 4.48 us -> none
where the time goes in v1:
time: 45 us; the launch traced here: 44.9 us
  Pallas kernels  44.1 us (98%)
  between operations  0.8 us (2%)
    pallas_call x1, Pallas kernels, per_device(): pl.pallas_call(functools.partial(kernel, n, members), out_shape=shapes, i...  43.3 us

profile of v1, /device:TPU:0, one launch (start us, length us, event | category | flops | bytes accessed | tf_op | source)
XLA Modules:
  0.0 44.9 jit_solution(3309332164500763573)
XLA Ops:
  0.6 43.3 %shard_map.121 = (f32[1,32,1024]{2,1,0:T(8,128)S(1)}, f32[1,32,1024]{2,1,0:T(8,128)S(1)}, f32[32,1024]{1,0:T(8,128)S(1)}) custom-call(f32[1,4]{1,0:T(1,128)} %par_hbm.1, f32[1,32,1024]{2,1,0:T(8,128)} %p_hbm.1, f32[1,32,1024]{2,1,0:T(8,128)} %q_hbm.1, f32[1,32,1024]{2,1,0:T(8,128)} %t_hbm.1, f32[32,3072]{1,0:T(8,128)} %v_hbm.1, f32[1,3072]{1,0:T(1,128)} %bitcast.4, ...), custom_call_target="tpu_custom_call" | custom-call | tf_op jit(solution)/shard_map/pallas_call | solution.py:568
  43.9 0.8 %shard_map.122 = (f32[1,32,1024]{2,1,0:T(8,128)}, f32[1,32,1024]{2,1,0:T(8,128)}, f32[32,1024]{1,0:T(8,128)}) custom-call(f32[1,32,1024]{2,1,0:T(8,128)S(1)} %get-tuple-element.6.p_hold, f32[1,32,1024]{2,1,0:T(8,128)S(1)} %get-tuple-element.7.t_hold, f32[32,1024]{1,0:T(8,128)S(1)} %get-tuple-element.8.e_hold), custom_call_target="tpu_custom_call" | custom-call | tf_op jit(solution)/shard_map/pallas_call | solution.py:638

commit v2 on v1

--- a/solution.py
+++ b/solution.py
@@ -11,7 +11,8 @@
 NS = 3
 TIME_STEP = 0.25
 LANES = 128
-CHUNKS = 2
+CHUNKS = 4
+GROUP = 2
 MESH = pl.DeviceIdType.MESH
 F32 = jnp.float32
 BF16 = jnp.bfloat16
@@ -93,6 +94,7 @@
     fin_ref,
     in_sem,
     out_sem,
+    exp_s,
     pick,
     g,
     m3,
@@ -129,8 +131,32 @@
     halo = nb * hb
     me = lax.axis_index("dom")
     mine = lax.axis_index("member")
+    stages = members.bit_length() - 1
+    groups = nb // GROUP
+    wide = GROUP * hb
+
     offsets = neighbour_offsets(nb)
-    stages = members.bit_length() - 1
+    ahead = [o for o in sorted(offsets, reverse=True) if o > 0]
+    behind = [o for o in sorted(offsets, reverse=True) if o < 0]
+    out_offsets = behind[1:] + behind[:1] + ahead
+    in_offsets = behind + ahead[-1:] + ahead[:-1]
+    out_blocks = [offsets.index(o) for o in out_offsets]
+    in_blocks = [offsets.index(o) for o in in_offsets]
+    half = (n + 1) // 2
+    upper = me // half
+
+    def turned(block):
+        return block + upper * (1 - 2 * (block % 2))
+
+    def meet(offset, block, order):
+        peer = lax.rem(me + offset * (1 - 2 * upper) + n * nb, n)
+        other = peer // half
+        differ = upper + other - 2 * upper * other
+        here, there = order.index(block), order.index(block + 1 - 2 * (block % 2))
+        return {"dom": peer}, here + differ * (there - here)
+
+    out_to = [meet(o, b, in_blocks) for o, b in zip(out_offsets, out_blocks)]
+    in_from = [meet(-o, b, out_blocks) for o, b in zip(in_offsets, in_blocks)]
 
     def dom_peer(k):
         return {"dom": lax.rem(me + (k % n), n)}
@@ -177,22 +203,35 @@
             device_id_type=MESH,
         )
 
-    def exchange(slot, chosen):
-        for b, offset in enumerate(offsets):
-            send[slot, b] = chosen[:, b * hb : (b + 1) * hb]
+    rows_of = [2] + [k % 2 for k in range(STEPS * NS)] + [3]
+
+    def exchange(slot, parts):
+        for t, (peer, place) in enumerate(out_to):
+            at = t % GROUP * hb
+            send[slot, t] = parts[t // GROUP][:, at : at + hb]
             to_peer(
-                send.at[slot, b],
-                recv.at[slot, b],
+                send.at[slot, t],
+                recv.at[slot, place],
                 send_sem.at[0],
-                recv_sem.at[slot],
-                dom_peer(offset),
+                recv_sem.at[rows_of[slot], place // GROUP],
+                peer,
             ).start()
 
-    def arrived(slot):
+    def arrived(slot, group):
+        at = slice(group * GROUP, (group + 1) * GROUP)
         to_peer(
-            send.at[slot], recv.at[slot], send_sem.at[0], recv_sem.at[slot], dom_peer(1)
+            send.at[slot, at],
+            recv.at[slot, at],
+            send_sem.at[0],
+            recv_sem.at[rows_of[slot], group],
+            dom_peer(1),
         ).wait_recv()
-        return halves(jnp.concatenate([recv[slot, b] for b in range(nb)], axis=1))
+        return halves(
+            jnp.concatenate([recv[slot, group * GROUP + i] for i in range(GROUP)], axis=1)
+        )
+
+    def parted(x):
+        return [x[:, at : at + wide] for at in range(0, halo, wide)]
 
     def chosen_of(*fields):
         y = mm(jnp.concatenate([halves(x) for x in fields], axis=0), pick[...])
@@ -200,7 +239,10 @@
 
     with scope("pick_build"):
         loads["exp"].wait()
-        one_hot(pick, blocks, halo, lambda cut: exp_ref[0:1, cut])
+        for t, block in enumerate(out_blocks):
+            at = pl.multiple_of(turned(block) * hb, hb)
+            exp_s[0:1, t * hb : (t + 1) * hb] = exp_ref[0:1, pl.ds(at, hb)]
+        one_hot(pick, blocks, halo, lambda cut: exp_s[0:1, cut])
     with scope("pick0"):
         loads["t"].wait()
         loads["p"].wait()
@@ -220,7 +262,15 @@
         couple = par_ref[0, 3]
         tab[0:8, :] = jnp.broadcast_to(met_ref[...], (8, slabs * cells))
         tab[8:16, :] = jnp.broadcast_to(ext_ref[...], (8, slabs * cells))
-        itab[...] = jnp.broadcast_to(fin_ref[1:2, :], (8, slabs * cells))
+        ends = fin_ref[1:2, :]
+        block = (ends >> 7) - blocks
+        block = block + upper * (1 - 2 * (block & 1))
+        place = block
+        for b in range(nb):
+            place = jnp.where(block == b, in_blocks.index(b), place)
+        inner = (ends >= cells) & (ends < cells + halo)
+        ends = jnp.where(inner, cells + place * hb + (ends & (hb - 1)), ends)
+        itab[...] = jnp.broadcast_to(ends, (8, slabs * cells))
 
         def slab(ref, rows, b, j):
             at = slabs * lax.broadcasted_iota(jnp.int32, (rows, LANES), 1) + j
@@ -251,8 +301,8 @@
     with scope("bar_wait"):
         pl.semaphore_wait(barrier, n - 1 + members - 1)
     with scope("send0"):
-        exchange(0, theta_s)
-        exchange(1, current_s)
+        exchange(0, parted(theta_s))
+        exchange(1, parted(current_s))
 
     with scope("g_build"):
         one_hot(g, (cells + halo) // LANES, slabs * cells, lambda cut: endj[0:1, cut])
@@ -270,8 +320,10 @@
         rows = jnp.concatenate(rows + [jnp.zeros((16 - 2 * slabs, cells), F32)], axis=0)
         y = fold(mm(halves(rows), pick[...]))
         for j in range(slabs):
-            ends_s[0:1, j * halo : (j + 1) * halo] = y[j : j + 1].astype(jnp.int32) - cells
-        weight_s = [y[slabs + j : slabs + j + 1] for j in range(slabs)]
+            for at, part in enumerate(parted(y[j : j + 1])):
+                lo = (at * slabs + j) * wide
+                ends_s[0:1, lo : lo + wide] = part.astype(jnp.int32) - cells
+        weight_s = [parted(y[slabs + j : slabs + j + 1]) for j in range(slabs)]
         one_hot(m3, nb, slabs * halo, lambda cut: ends_s[0:1, cut])
 
     def local(pressure, heat=None):
@@ -295,8 +347,31 @@
     def far(x, j):
         return mm(x, g[cells:, cuts[j]])
 
-    def far_s(x, j):
-        return mm(x, m3[:, j * halo : (j + 1) * halo])
+    def relay(slot, parts, weights):
+        held = []
+        for group in range(groups):
+            x = arrived(slot, group)
+            held.append(x)
+            found = [
+                mm(
+                    x,
+                    m3[
+                        group * wide : (group + 1) * wide,
+                        part * slabs * wide : (part + 1) * slabs * wide,
+                    ],
+                )
+                for part in range(groups)
+            ]
+            for part, y in enumerate(found):
+                y = fold(y)
+                for j in range(slabs):
+                    parts[part] = parts[part] + weights[j][part] * (
+                        y[:, j * wide : (j + 1) * wide]
+                    )
+        return parts, jnp.concatenate(held, axis=1)
+
+    def arrived_all(slot):
+        return jnp.concatenate([arrived(slot, group) for group in range(groups)], axis=1)
 
     def heat_base(heat, div):
         step = heat[1:] - heat[:-1]
@@ -353,22 +428,19 @@
         t_base = heat_base(theta, t_sum)
     with scope("base_0"):
         base_s, t_base_s, *turn_s = chosen_of(
-            base, t_base, *[rate * cf[j] for j in range(slabs)]
+            base, t_base, *[-rate * cf[j] for j in range(slabs)]
         )
+    share = couple / NS
     with scope("wait_0"):
-        ht = arrived(0)
-        hp = arrived(1)
-    share = couple / NS
-    with scope("crit_0"):
-        both = jnp.concatenate([ht, hp], axis=0)
-        out, t_out_s = base_s, t_base_s
-        for j in range(slabs):
-            y = far_s(both, j)
-            t_out_s = t_out_s - turn_s[j] * fold(y[: 2 * levels])
-            out = out + weight_s[j] * fold(y[2 * levels :])
-        out = out + share * (t_out_s - theta_s)
+        t_out_s, ht = relay(0, parted(t_base_s), [parted(x) for x in turn_s])
+        base_s = [
+            x + share * (new - old)
+            for x, new, old in zip(parted(base_s), t_out_s, parted(theta_s))
+        ]
+        out, hp = relay(1, base_s, weight_s)
         exchange(2, out)
         exchange(STEPS * NS + 1, t_out_s)
+        both = jnp.concatenate([ht, hp], axis=0)
     with scope("full_0"):
         theta1 = t_base
         previous, stepped = current, base
@@ -379,15 +451,19 @@
         forcing = share * (theta1 - theta)
         current = stepped + forcing
 
-    def w_copy(b, offset):
-        whole = offset == 0
-        return to_peer(
-            w_send if whole else w_send.at[b],
-            w_recv if whole else w_recv.at[b],
-            w_sem.at[0],
-            w_sem.at[1],
-            dom_peer(1 if whole else offset),
-        )
+    w_all = to_peer(w_send, w_recv, w_sem.at[0], w_sem.at[1], dom_peer(1))
+
+    def pull(places):
+        rows = jnp.concatenate([speed * m for m in metric], axis=1)
+        rows = halves(jnp.broadcast_to(rows, (16, slabs * cells)))
+        lo, hi = cells + places[0] * hb, cells + (places[-1] + 1) * hb
+        w = fold(mm_nt(rows, g[lo:hi, :]))
+        for i, u in enumerate(places):
+            peer, place = in_from[u]
+            w_send[u] = w[0:8, i * hb : (i + 1) * hb]
+            to_peer(
+                w_send.at[u], w_recv.at[place], w_sem.at[0], w_sem.at[1], peer
+            ).start()
 
     total = STEPS * NS
     for k in range(1, total):
@@ -398,7 +474,7 @@
             else:
                 p_sum = local(current)
             if k == NS - 1:
-                ht = arrived(STEPS * NS + 1)
+                ht = arrived_all(STEPS * NS + 1)
                 theta2 = t_base
                 for j in range(slabs):
                     theta2 = theta2 - rate * (cf[j] * fold(far(ht, j)))
@@ -414,33 +490,25 @@
         if k < total - 1:
             with scope(f"base_{k}"):
                 (base_s,) = chosen_of(base)
+                base_s = parted(base_s)
         else:
             with scope("mean_1"):
-                w_copy(0, 0).wait_recv()
+                w_all.wait_recv()
                 weighted = lane_blocks(base * area)
                 for b in range(nb):
                     weighted = weighted + w_recv[b, 0:1] * send[k + 1, b]
                 partial_mean(1, weighted)
                 first_row = mean_row(0)
                 first = as_column(first_row)
-        if k == NS:
-            with scope("pull"):
-                rows = jnp.concatenate(
-                    [speed * m for m in metric], axis=1
-                )
-                rows = halves(jnp.broadcast_to(rows, (16, slabs * cells)))
-                w = fold(mm_nt(rows, g[cells:, :]))
-                for b, offset in enumerate(offsets):
-                    w_send[b] = w[0:8, b * hb : (b + 1) * hb]
-                    w_copy(b, -offset).start()
+        if k in (1, NS):
+            with scope(f"pull_{k}"):
+                pull(range(nb // 2) if k == 1 else range(nb // 2, nb))
         with scope(f"wait_{k}"):
-            hp = arrived(k + 1)
-        if k < total - 1:
-            with scope(f"crit_{k}"):
-                out = base_s
-                for j in range(slabs):
-                    out = out + weight_s[j] * fold(far_s(hp, j))
+            if k < total - 1:
+                out, hp = relay(k + 1, base_s, weight_s)
                 exchange(k + 2, out)
+            else:
+                hp = arrived_all(k + 1)
         with scope(f"full_{k}"):
             previous, stepped = current, base
             for j in range(slabs):
@@ -503,9 +571,9 @@
         e_copy = pltpu.make_async_copy(e_out, e_hold, out_sem.at[2])
         e_copy.start()
     with scope("drain"):
-        to_peer(send, recv, send_sem.at[0], recv_sem.at[0], dom_peer(1)).wait_send()
+        to_peer(send, recv, send_sem.at[0], recv_sem.at[0, 0], dom_peer(1)).wait_send()
         to_peer(mean_recv, mean_recv, mean_ssem.at[0], mean_rsem.at[0], dom_peer(1)).wait_send()
-        w_copy(0, 0).wait_send()
+        w_all.wait_send()
         if stages:
             to_peer(
                 mem_send, mem_recv, mem_ssem.at[0], mem_rsem.at[0, 0], partner(0)
@@ -586,6 +654,7 @@
                 pltpu.VMEM((2, edges), jnp.int32),
                 dma((10,)),
                 dma((3,)),
+                pltpu.VMEM((1, halo), jnp.int32),
                 pltpu.VMEM((cells, halo), F8),
                 pltpu.VMEM((cells + halo, edges), F8),
                 pltpu.VMEM((halo, slabs * halo), F8),
@@ -607,7 +676,7 @@
                 pltpu.VMEM((nb, 8, hb), F32),
                 pltpu.VMEM((nb, 8, hb), F32),
                 dma((1,)),
-                dma((slots,)),
+                dma((4, nb // GROUP)),
                 dma((1,)),
                 dma((STEPS,)),
                 dma((1,)),

time: 45 us -> 43.3 us (0.962)
  Pallas kernels: 44.1 us -> 42.4 us
    pallas_call x1, Pallas kernels: 43.3 us -> 41.6 us  [per_device(): pl.pallas_call(functools.partial(kernel, n, members), out_shape=shapes, i...]
where the time goes in v2:
time: 43.3 us; the launch traced here: 43.2 us
  Pallas kernels  42.4 us (98%)
  between operations  0.8 us (2%)
    pallas_call x1, Pallas kernels, per_device(): pl.pallas_call(functools.partial(kernel, n, members), out_shape=shapes, i...  41.6 us

profile of v2, /device:TPU:0, one launch (start us, length us, event | category | flops | bytes accessed | tf_op | source)
XLA Modules:
  0.0 43.2 jit_solution(18403128928290440227)
XLA Ops:
  0.6 41.6 %shard_map.121 = (f32[1,32,1024]{2,1,0:T(8,128)S(1)}, f32[1,32,1024]{2,1,0:T(8,128)S(1)}, f32[32,1024]{1,0:T(8,128)S(1)}) custom-call(f32[1,4]{1,0:T(1,128)} %par_hbm.1, f32[1,32,1024]{2,1,0:T(8,128)} %p_hbm.1, f32[1,32,1024]{2,1,0:T(8,128)} %q_hbm.1, f32[1,32,1024]{2,1,0:T(8,128)} %t_hbm.1, f32[32,3072]{1,0:T(8,128)} %v_hbm.1, f32[1,3072]{1,0:T(1,128)} %bitcast.4, ...), custom_call_target="tpu_custom_call" | custom-call | tf_op jit(solution)/shard_map/pallas_call | solution.py:636
  42.2 0.8 %shard_map.122 = (f32[1,32,1024]{2,1,0:T(8,128)}, f32[1,32,1024]{2,1,0:T(8,128)}, f32[32,1024]{1,0:T(8,128)}) custom-call(f32[1,32,1024]{2,1,0:T(8,128)S(1)} %get-tuple-element.6.p_hold, f32[1,32,1024]{2,1,0:T(8,128)S(1)} %get-tuple-element.7.t_hold, f32[32,1024]{1,0:T(8,128)S(1)} %get-tuple-element.8.e_hold), custom_call_target="tpu_custom_call" | custom-call | tf_op jit(solution)/shard_map/pallas_call | solution.py:707

commit v3 on v2

--- a/solution.py
+++ b/solution.py
@@ -115,6 +115,10 @@
     mm_recv,
     w_send,
     w_recv,
+    en_send,
+    en_recv,
+    en_sum,
+    eh,
     send_sem,
     recv_sem,
     mean_ssem,
@@ -123,6 +127,9 @@
     mem_rsem,
     mm_sem,
     w_sem,
+    en_sem,
+    ready_sem,
+    fence_sem,
 ):
     levels, cells = p_ref.shape[1], p_ref.shape[2]
     slabs = v_ref.shape[1] // cells
@@ -133,6 +140,8 @@
     mine = lax.axis_index("member")
     stages = members.bit_length() - 1
     groups = nb // GROUP
+    lead = nb - GROUP
+    spans = [(0, lead), (lead, nb)] if lead else [(0, nb)]
     wide = GROUP * hb
 
     offsets = neighbour_offsets(nb)
@@ -205,30 +214,37 @@
 
     rows_of = [2] + [k % 2 for k in range(STEPS * NS)] + [3]
 
-    def exchange(slot, parts):
-        for t, (peer, place) in enumerate(out_to):
+    def give(slot, part, x):
+        for t in range(part * GROUP, (part + 1) * GROUP):
+            peer, place = out_to[t]
             at = t % GROUP * hb
-            send[slot, t] = parts[t // GROUP][:, at : at + hb]
+            send[slot, t] = x[:, at : at + hb]
             to_peer(
                 send.at[slot, t],
                 recv.at[slot, place],
                 send_sem.at[0],
-                recv_sem.at[rows_of[slot], place // GROUP],
+                recv_sem.at[rows_of[slot], place // lead if lead else 0],
                 peer,
             ).start()
 
+    def fence():
+        pl.semaphore_signal(fence_sem, 1)
+        pl.semaphore_wait(fence_sem, 1)
+
+    def exchange(slot, parts):
+        for part, x in enumerate(parts):
+            give(slot, part, x)
+
     def arrived(slot, group):
-        at = slice(group * GROUP, (group + 1) * GROUP)
+        lo, hi = spans[group]
         to_peer(
-            send.at[slot, at],
-            recv.at[slot, at],
+            send.at[slot, lo:hi],
+            recv.at[slot, lo:hi],
             send_sem.at[0],
             recv_sem.at[rows_of[slot], group],
             dom_peer(1),
         ).wait_recv()
-        return halves(
-            jnp.concatenate([recv[slot, group * GROUP + i] for i in range(GROUP)], axis=1)
-        )
+        return halves(jnp.concatenate([recv[slot, u] for u in range(lo, hi)], axis=1))
 
     def parted(x):
         return [x[:, at : at + wide] for at in range(0, halo, wide)]
@@ -304,6 +320,9 @@
         exchange(0, parted(theta_s))
         exchange(1, parted(current_s))
 
+        for k in range(1, members):
+            pl.semaphore_signal(ready_sem, inc=1, device_id=member_peer(k), device_id_type=MESH)
+
     with scope("g_build"):
         one_hot(g, (cells + halo) // LANES, slabs * cells, lambda cut: endj[0:1, cut])
     with scope("coef"):
@@ -347,31 +366,27 @@
     def far(x, j):
         return mm(x, g[cells:, cuts[j]])
 
-    def relay(slot, parts, weights):
+    def relay(slot, parts, weights, to=None):
         held = []
-        for group in range(groups):
+        parts = list(parts)
+        for group, (lo, hi) in enumerate(spans):
             x = arrived(slot, group)
             held.append(x)
-            found = [
-                mm(
-                    x,
-                    m3[
-                        group * wide : (group + 1) * wide,
-                        part * slabs * wide : (part + 1) * slabs * wide,
-                    ],
-                )
-                for part in range(groups)
-            ]
+            found = []
+            for part in range(groups):
+                at = part * slabs * wide
+                found.append(mm(x, m3[lo * hb : hi * hb, at : at + slabs * wide]))
             for part, y in enumerate(found):
-                y = fold(y)
                 for j in range(slabs):
-                    parts[part] = parts[part] + weights[j][part] * (
+                    parts[part] = parts[part] + weights[j][part] * fold(
                         y[:, j * wide : (j + 1) * wide]
                     )
+                if to is not None and hi == nb:
+                    give(to, part, parts[part])
         return parts, jnp.concatenate(held, axis=1)
 
     def arrived_all(slot):
-        return jnp.concatenate([arrived(slot, group) for group in range(groups)], axis=1)
+        return jnp.concatenate([arrived(slot, i) for i in range(len(spans))], axis=1)
 
     def heat_base(heat, div):
         step = heat[1:] - heat[:-1]
@@ -402,6 +417,7 @@
                 mean_rsem.at[slot],
                 dom_peer(k),
             ).start()
+        return row
 
     def mean_row(slot):
         to_peer(
@@ -437,9 +453,9 @@
             x + share * (new - old)
             for x, new, old in zip(parted(base_s), t_out_s, parted(theta_s))
         ]
-        out, hp = relay(1, base_s, weight_s)
-        exchange(2, out)
+        _, hp = relay(1, base_s, weight_s, 2)
         exchange(STEPS * NS + 1, t_out_s)
+        fence()
         both = jnp.concatenate([ht, hp], axis=0)
     with scope("full_0"):
         theta1 = t_base
@@ -465,22 +481,73 @@
                 w_send.at[u], w_recv.at[place], w_sem.at[0], w_sem.at[1], peer
             ).start()
 
+    layer = levels // members
+    en_all = to_peer(en_recv, en_recv, en_sem.at[0], en_sem.at[1], member_peer(1))
+    eh_all = to_peer(eh, eh, en_sem.at[2], en_sem.at[3], dom_peer(1))
+
+    def gather_exports(parts):
+        for t in range(nb):
+            at = t % GROUP * hb
+            x = speed * parts[t // GROUP][:, at : at + hb]
+            for m in range(members):
+                en_send[m, t] = x[m * layer : (m + 1) * layer]
+        for k in range(1, members):
+            to = lax.rem(mine + k, members)
+            to_peer(
+                en_send.at[to], en_recv.at[k - 1], en_sem.at[0], en_sem.at[1], {"member": to}
+            ).start()
+
+    def spread_exports():
+        if members > 1:
+            en_all.wait_recv()
+        summed = en_send[mine]
+        for k in range(members - 1):
+            summed = summed + en_recv[k]
+        en_sum[...] = summed
+        rows = pl.ds(pl.multiple_of(mine * layer, layer), layer)
+        for t, (peer, place) in enumerate(out_to):
+            for k in range(members):
+                to_peer(
+                    en_sum.at[t],
+                    eh.at[place, rows],
+                    en_sem.at[2],
+                    en_sem.at[3],
+                    {**peer, "member": lax.rem(mine + k, members)},
+                ).start()
+
+    some = max(stages, 1)
+    pieces = some * CHUNKS
+    width = cells // pieces
+
+    def member_copy(stage, c):
+        return to_peer(
+            mem_send.at[stage, c],
+            mem_recv.at[stage, c],
+            mem_ssem.at[0],
+            mem_rsem.at[stage, c // some],
+            partner((stage + c) % some),
+        )
+
+    def chunk_wait(stage, group):
+        at = slice(group * some, (group + 1) * some)
+        to_peer(
+            mem_send.at[stage, at],
+            mem_recv.at[stage, at],
+            mem_ssem.at[0],
+            mem_rsem.at[stage, group],
+            partner(0),
+        ).wait_recv()
+
     total = STEPS * NS
     for k in range(1, total):
+        if k == total - 2 and members > 1:
+            pl.semaphore_wait(ready_sem, members - 1)
         with scope(f"local_{k}"):
             if k == 1:
                 p_sum, t_sum = local(current, theta1)
                 t_base = heat_base(theta1, t_sum)
             else:
                 p_sum = local(current)
-            if k == NS - 1:
-                ht = arrived_all(STEPS * NS + 1)
-                theta2 = t_base
-                for j in range(slabs):
-                    theta2 = theta2 - rate * (cf[j] * fold(far(ht, j)))
-                t_out[0] = theta2
-                t_copy = pltpu.make_async_copy(t_out, t_hold, out_sem.at[0])
-                t_copy.start()
             if k == NS:
                 forcing = share * (theta2 - theta1)
                 partial_mean(0, lane_blocks(current * area))
@@ -492,21 +559,48 @@
                 (base_s,) = chosen_of(base)
                 base_s = parted(base_s)
         else:
+            with scope("bulk"):
+                for c in range(pieces):
+                    mem_send[0, c] = base[:, c * width : (c + 1) * width]
+                    if stages:
+                        member_copy(0, c).start()
             with scope("mean_1"):
                 w_all.wait_recv()
                 weighted = lane_blocks(base * area)
                 for b in range(nb):
                     weighted = weighted + w_recv[b, 0:1] * send[k + 1, b]
-                partial_mean(1, weighted)
+                mm_send[...] = partial_mean(1, weighted)
+                for m in range(1, members):
+                    for d in range(n):
+                        to_peer(
+                            mm_send,
+                            mm_recv.at[m - 1, d],
+                            mm_sem.at[0],
+                            mm_sem.at[1],
+                            {**dom_peer(d), **member_peer(m)},
+                        ).start()
                 first_row = mean_row(0)
                 first = as_column(first_row)
+            with scope("spread"):
+                spread_exports()
+        if k == NS - 1:
+            with scope("heat_2"):
+                ht = arrived_all(STEPS * NS + 1)
+                theta2 = t_base
+                for j in range(slabs):
+                    theta2 = theta2 - rate * (cf[j] * fold(far(ht, j)))
+                t_out[0] = theta2
+                t_copy = pltpu.make_async_copy(t_out, t_hold, out_sem.at[0])
+                t_copy.start()
         if k in (1, NS):
             with scope(f"pull_{k}"):
                 pull(range(nb // 2) if k == 1 else range(nb // 2, nb))
         with scope(f"wait_{k}"):
             if k < total - 1:
-                out, hp = relay(k + 1, base_s, weight_s)
-                exchange(k + 2, out)
+                out, hp = relay(k + 1, base_s, weight_s, k + 2)
+                if k == total - 2:
+                    gather_exports(out)
+                fence()
             else:
                 hp = arrived_all(k + 1)
         with scope(f"full_{k}"):
@@ -515,65 +609,53 @@
                 stepped = stepped + (scale * metric[j]) * fold(far(hp, j))
             current = stepped
 
-    with scope("tail_send"):
-        current = jnp.where(owned, current - first, current)
-        pieces = max(stages, 1) * CHUNKS
-        width = cells // pieces
-
-        def member_copy(stage, c):
-            return to_peer(
-                mem_send.at[stage, c],
-                mem_recv.at[stage, c],
-                mem_ssem.at[0],
-                mem_rsem.at[stage, c],
-                partner((stage + c) % max(stages, 1)),
-            )
-
-        def row_copy(k):
-            return to_peer(
-                mm_send, mm_recv.at[k - 1], mm_sem.at[0], mm_sem.at[1], member_peer(k)
-            )
-
-        for c in range(pieces):
-            mem_send[0, c] = current[:, c * width : (c + 1) * width]
-            if stages:
-                member_copy(0, c).start()
-    with scope("tail_mean"):
-        last = mean_row(1) - first_row
-        mm_send[...] = last
-        for k in range(1, members):
-            row_copy(k).start()
-        column = as_column(last)
-        p_out[0] = jnp.where(owned, current - column, current)
-        p_copy = pltpu.make_async_copy(p_out, p_hold, out_sem.at[1])
-        p_copy.start()
     for s in range(stages - 1):
         with scope(f"tail_stage_{s}"):
             for c in range(pieces):
-                member_copy(s, c).wait_recv()
+                if c % some == 0:
+                    chunk_wait(s, c // some)
                 mem_send[s + 1, c] = mem_send[s, c] + mem_recv[s, c]
                 member_copy(s + 1, c).start()
+    with scope("tail_mean"):
+        current = jnp.where(owned, current - first, current)
+        last = mean_row(1) - first_row
+        p_out[0] = jnp.where(owned, current - as_column(last), current)
+        p_copy = pltpu.make_async_copy(p_out, p_hold, out_sem.at[1])
+        p_copy.start()
+    with scope("tail_far"):
+        eh_all.wait_recv()
+        x = halves(jnp.concatenate([eh[u] for u in range(nb)], axis=1))
+        field = jnp.zeros((levels, cells), F32)
+        for j in range(slabs):
+            field = field + jnp.where(owned, inverse * metric[j], 0.0) * fold(far(x, j))
     with scope("tail_rows"):
-        summed = last
+        summed = (first_row + last)[0:1]
         if members > 1:
             to_peer(mm_recv, mm_recv, mm_sem.at[0], mm_sem.at[1], member_peer(1)).wait_recv()
-            for k in range(members - 1):
-                summed = summed + mm_recv[k]
-        column = as_column(summed)
+            for m in range(members - 1):
+                row = mm_recv[m, 0]
+                for d in range(1, n):
+                    row = row + mm_recv[m, d]
+                summed = summed + row / row[:, levels : levels + 1]
+        field = field - jnp.where(owned, as_column(summed), 0.0)
     with scope("tail_end"):
         for c in range(pieces):
             cut = slice(c * width, (c + 1) * width)
-            field = mem_send[max(stages - 1, 0), c]
+            x = mem_send[some - 1, c]
             if stages:
-                member_copy(stages - 1, c).wait_recv()
-                field = field + mem_recv[stages - 1, c]
-            e_out[:, cut] = (field - jnp.where(owned[:, cut], column, 0.0)) / members
+                if c % some == 0:
+                    chunk_wait(stages - 1, c // some)
+                x = x + mem_recv[stages - 1, c]
+            e_out[:, cut] = (x + field[:, cut]) / members
         e_copy = pltpu.make_async_copy(e_out, e_hold, out_sem.at[2])
         e_copy.start()
     with scope("drain"):
         to_peer(send, recv, send_sem.at[0], recv_sem.at[0, 0], dom_peer(1)).wait_send()
         to_peer(mean_recv, mean_recv, mean_ssem.at[0], mean_rsem.at[0], dom_peer(1)).wait_send()
         w_all.wait_send()
+        if members > 1:
+            en_all.wait_send()
+        eh_all.wait_send()
         if stages:
             to_peer(
                 mem_send, mem_recv, mem_ssem.at[0], mem_rsem.at[0, 0], partner(0)
@@ -671,18 +753,25 @@
                 pltpu.VMEM((STEPS, n - 1, 8, LANES), F32),
                 pltpu.VMEM((some, pieces, levels, cells // pieces), F32),
                 pltpu.VMEM((some, pieces, levels, cells // pieces), F32),
-                pltpu.VMEM((8, LANES), F32),
-                pltpu.VMEM((max(members - 1, 1), 8, LANES), F32),
+                pltpu.VMEM((1, LANES), F32),
+                pltpu.VMEM((max(members - 1, 1), n, 1, LANES), F32),
                 pltpu.VMEM((nb, 8, hb), F32),
                 pltpu.VMEM((nb, 8, hb), F32),
+                pltpu.VMEM((members, nb, levels // members, hb), F32),
+                pltpu.VMEM((max(members - 1, 1), nb, levels // members, hb), F32),
+                pltpu.VMEM((nb, levels // members, hb), F32),
+                pltpu.VMEM((nb, levels, hb), F32),
                 dma((1,)),
-                dma((4, nb // GROUP)),
+                dma((4, 2)),
                 dma((1,)),
                 dma((STEPS,)),
                 dma((1,)),
-                dma((some, pieces)),
+                dma((some, CHUNKS)),
                 dma((2,)),
                 dma((2,)),
+                dma((4,)),
+                pltpu.SemaphoreType.REGULAR,
+                pltpu.SemaphoreType.REGULAR,
             ],
             compiler_params=pltpu.CompilerParams(
                 collective_id=0, has_side_effects=True, vmem_limit_bytes=32 * 1024 * 1024

time: 43.3 us -> 41.1 us (0.949)
  Pallas kernels: 42.4 us -> 40.2 us
    pallas_call x1, Pallas kernels: 41.6 us -> 39.4 us  [per_device(): pl.pallas_call(functools.partial(kernel, n, members), out_shape=shapes, i...]
where the time goes in v3:
time: 41.1 us; the launch traced here: 41 us
  Pallas kernels  40.2 us (98%)
  between operations  0.8 us (2%)
    pallas_call x1, Pallas kernels, per_device(): pl.pallas_call(functools.partial(kernel, n, members), out_shape=shapes, i...  39.4 us

profile of v3, /device:TPU:0, one launch (start us, length us, event | category | flops | bytes accessed | tf_op | source)
XLA Modules:
  0.0 41.0 jit_solution(11967103980241894601)
XLA Ops:
  0.6 39.4 %shard_map.121 = (f32[1,32,1024]{2,1,0:T(8,128)S(1)}, f32[1,32,1024]{2,1,0:T(8,128)S(1)}, f32[32,1024]{1,0:T(8,128)S(1)}) custom-call(f32[1,4]{1,0:T(1,128)} %par_hbm.1, f32[1,32,1024]{2,1,0:T(8,128)} %p_hbm.1, f32[1,32,1024]{2,1,0:T(8,128)} %q_hbm.1, f32[1,32,1024]{2,1,0:T(8,128)} %t_hbm.1, f32[32,3072]{1,0:T(8,128)} %v_hbm.1, f32[1,3072]{1,0:T(1,128)} %bitcast.4, ...), custom_call_target="tpu_custom_call" | custom-call | tf_op jit(solution)/shard_map/pallas_call | solution.py:718
  40.0 0.8 %shard_map.122 = (f32[1,32,1024]{2,1,0:T(8,128)}, f32[1,32,1024]{2,1,0:T(8,128)}, f32[32,1024]{1,0:T(8,128)}) custom-call(f32[1,32,1024]{2,1,0:T(8,128)S(1)} %get-tuple-element.6.p_hold, f32[1,32,1024]{2,1,0:T(8,128)S(1)} %get-tuple-element.7.t_hold, f32[32,1024]{1,0:T(8,128)S(1)} %get-tuple-element.8.e_hold), custom_call_target="tpu_custom_call" | custom-call | tf_op jit(solution)/shard_map/pallas_call | solution.py:796

commit v4 on v3

--- a/solution.py
+++ b/solution.py
@@ -264,7 +264,7 @@
         loads["p"].wait()
         current = p_ref[0]
         theta = t_ref[0]
-        theta_s, current_s = chosen_of(theta, current)
+        (theta_s,) = chosen_of(theta)
 
     with scope("tables"):
         loads["fin"].wait()
@@ -318,6 +318,7 @@
         pl.semaphore_wait(barrier, n - 1 + members - 1)
     with scope("send0"):
         exchange(0, parted(theta_s))
+        (current_s,) = chosen_of(current)
         exchange(1, parted(current_s))
 
         for k in range(1, members):
@@ -448,15 +449,26 @@
         )
     share = couple / NS
     with scope("wait_0"):
-        t_out_s, ht = relay(0, parted(t_base_s), [parted(x) for x in turn_s])
-        base_s = [
-            x + share * (new - old)
-            for x, new, old in zip(parted(base_s), t_out_s, parted(theta_s))
-        ]
-        _, hp = relay(1, base_s, weight_s, 2)
+        turn_s = [parted(x) for x in turn_s]
+        t_out_s, out, theta_s = parted(t_base_s), parted(base_s), parted(theta_s)
+        held = []
+        for group, (lo, hi) in enumerate(spans):
+            x = jnp.concatenate([arrived(0, group), arrived(1, group)], axis=0)
+            held.append(x)
+            found = []
+            for part in range(groups):
+                at = part * slabs * wide
+                found.append(mm(x, m3[lo * hb : hi * hb, at : at + slabs * wide]))
+            for part, y in enumerate(found):
+                for j in range(slabs):
+                    cut = slice(j * wide, (j + 1) * wide)
+                    t_out_s[part] = t_out_s[part] + turn_s[j][part] * fold(y[: 2 * levels, cut])
+                    out[part] = out[part] + weight_s[j][part] * fold(y[2 * levels :, cut])
+                if hi == nb:
+                    give(2, part, out[part] + share * (t_out_s[part] - theta_s[part]))
         exchange(STEPS * NS + 1, t_out_s)
         fence()
-        both = jnp.concatenate([ht, hp], axis=0)
+        both = jnp.concatenate(held, axis=1)
     with scope("full_0"):
         theta1 = t_base
         previous, stepped = current, base
@@ -482,6 +494,15 @@
             ).start()
 
     layer = levels // members
+    away = sorted(range(members), key=lambda x: (-bin(x).count("1"), x))
+
+    def member_at(x):
+        other = mine
+        for stage in range(stages):
+            if x >> stage & 1:
+                bit = 1 << stage
+                other = other + bit - 2 * bit * lax.rem(mine // bit, 2)
+        return other
     en_all = to_peer(en_recv, en_recv, en_sem.at[0], en_sem.at[1], member_peer(1))
     eh_all = to_peer(eh, eh, en_sem.at[2], en_sem.at[3], dom_peer(1))
 
@@ -491,10 +512,10 @@
             x = speed * parts[t // GROUP][:, at : at + hb]
             for m in range(members):
                 en_send[m, t] = x[m * layer : (m + 1) * layer]
-        for k in range(1, members):
-            to = lax.rem(mine + k, members)
+        for x in away[:-1]:
+            to = member_at(x)
             to_peer(
-                en_send.at[to], en_recv.at[k - 1], en_sem.at[0], en_sem.at[1], {"member": to}
+                en_send.at[to], en_recv.at[x - 1], en_sem.at[0], en_sem.at[1], {"member": to}
             ).start()
 
     def spread_exports():
@@ -506,13 +527,13 @@
         en_sum[...] = summed
         rows = pl.ds(pl.multiple_of(mine * layer, layer), layer)
         for t, (peer, place) in enumerate(out_to):
-            for k in range(members):
+            for x in away:
                 to_peer(
                     en_sum.at[t],
                     eh.at[place, rows],
                     en_sem.at[2],
                     en_sem.at[3],
-                    {**peer, "member": lax.rem(mine + k, members)},
+                    {**peer, "member": member_at(x)},
                 ).start()
 
     some = max(stages, 1)

time: 41.1 us -> 42 us (1.022)
  Pallas kernels: 40.2 us -> 40.8 us
    pallas_call x1, Pallas kernels: 39.4 us -> 40.1 us  [per_device(): pl.pallas_call(functools.partial(kernel, n, members), out_shape=shapes, i...]
where the time goes in v4:
time: 42 us; the launch traced here: 41.6 us
  Pallas kernels  40.8 us (97%)
  between operations  0.8 us (2%)
    pallas_call x1, Pallas kernels, per_device(): pl.pallas_call(functools.partial(kernel, n, members), out_shape=shapes, i...  40.1 us

profile of v4, /device:TPU:0, one launch (start us, length us, event | category | flops | bytes accessed | tf_op | source)
XLA Modules:
  0.0 41.6 jit_solution(8162463828998476764)
XLA Ops:
  0.6 40.1 %shard_map.121 = (f32[1,32,1024]{2,1,0:T(8,128)S(1)}, f32[1,32,1024]{2,1,0:T(8,128)S(1)}, f32[32,1024]{1,0:T(8,128)S(1)}) custom-call(f32[1,4]{1,0:T(1,128)} %par_hbm.1, f32[1,32,1024]{2,1,0:T(8,128)} %p_hbm.1, f32[1,32,1024]{2,1,0:T(8,128)} %q_hbm.1, f32[1,32,1024]{2,1,0:T(8,128)} %t_hbm.1, f32[32,3072]{1,0:T(8,128)} %v_hbm.1, f32[1,3072]{1,0:T(1,128)} %bitcast.4, ...), custom_call_target="tpu_custom_call" | custom-call | tf_op jit(solution)/shard_map/pallas_call | solution.py:739
  40.7 0.8 %shard_map.122 = (f32[1,32,1024]{2,1,0:T(8,128)}, f32[1,32,1024]{2,1,0:T(8,128)}, f32[32,1024]{1,0:T(8,128)}) custom-call(f32[1,32,1024]{2,1,0:T(8,128)S(1)} %get-tuple-element.6.p_hold, f32[1,32,1024]{2,1,0:T(8,128)S(1)} %get-tuple-element.7.t_hold, f32[32,1024]{1,0:T(8,128)S(1)} %get-tuple-element.8.e_hold), custom_call_target="tpu_custom_call" | custom-call | tf_op jit(solution)/shard_map/pallas_call | solution.py:817
